TPU v7x, 32 devices: a whole 2x2x4 slice. The times are simulated.
32 devices in a mesh: dp: 4 (over y, core), expert: 4 (over z), tensor: 2 (over x).
Axes of the slice: x: 2, y: 2, z: 4, core: 2. Of those that a mesh axis runs over, the one named last changes fastest.
Arguments:
- tokens: bfloat16 [96, 7168], P('expert', 'tensor'), may hold values from -6 to 6
- expert_ids: int32 [96, 8], P('expert'), may hold values from 0 to 63, all different within a row; in each aligned block of 24 rows (0 to 23, 24 to 47, ...) at most 4 rows name the same one
- gate_weights: float32 [96, 8], P('expert'), may hold values from 0.1 to 1
- w_gate: bfloat16 [64, 7168, 1024], P('expert', 'tensor', 'dp'), may hold values from -0.0625 to 0.0625
- w_up: bfloat16 [64, 7168, 1024], P('expert', 'tensor', 'dp'), may hold values from -0.0625 to 0.0625
- w_down: bfloat16 [64, 1024, 7168], P('expert', 'dp', 'tensor'), may hold values from -0.1875 to 0.1875
Outputs:
- mixed: bfloat16 [96, 7168], P('expert', 'tensor')
Inputs may be any that keep to these rules, and one draw needn't show every extreme that they name: `expert_ids`: each row names 8 different experts. Among the rows of one index of the expert axis (aligned blocks of 24 rows) no expert is named more than 4 times, and in some block one expert is named exactly 4 times.
All inputs are finite; a program needn't handle non-finite values.
Results may differ from a plain program's by a relative error of at most 0.0049.
Values may be sent and summed in bfloat16 or wider, within the bound.
A program may use at most 128 MiB of HBM per device.

v0:
```python
import jax
import jax.numpy as jnp
from jax import lax
from jax.sharding import PartitionSpec as P

TOP = 8
CAP = 4


def per_device(tokens, expert_ids, gate_weights, w_gate, w_up, w_down):
    expert_count = lax.axis_size("expert")
    hidden_count = lax.axis_size("dp")
    local_experts = w_gate.shape[0]
    tok_rows = tokens.shape[0]
    feature_cols = tokens.shape[1]
    total_experts = local_experts * expert_count
    cap_share = CAP // hidden_count
    slot_total = local_experts * CAP * expert_count
    flat_ids = expert_ids.reshape(-1)
    one_hot = (flat_ids[:, None] == lax.iota(jnp.int32, total_experts)[None, :]).astype(jnp.int32)
    earlier = jnp.cumsum(one_hot, axis=0) - one_hot
    slot_rank = jnp.sum(earlier * one_hot, axis=1)
    owner_device = flat_ids // local_experts
    within = flat_ids % local_experts
    send_slot = (within * CAP + slot_rank) * expert_count + owner_device
    dispatch_table = (send_slot[None, :] == lax.iota(jnp.int32, slot_total)[:, None]).astype(
        jnp.float32
    )
    dispatch_table = jnp.sum(dispatch_table.reshape(slot_total, tok_rows, TOP), axis=2).astype(
        jnp.bfloat16
    )
    outbound = jnp.dot(dispatch_table, tokens, preferred_element_type=jnp.float32).astype(
        jnp.bfloat16
    )
    outbound = outbound.reshape(local_experts, CAP, expert_count, feature_cols)
    arrived = lax.all_to_all(outbound, "expert", split_axis=2, concat_axis=2, tiled=True)
    expert_rows = arrived.reshape(local_experts, CAP * expert_count, feature_cols)
    gate_part = jnp.einsum("lrd,ldf->lrf", expert_rows, w_gate, preferred_element_type=jnp.float32)
    up_part = jnp.einsum("lrd,ldf->lrf", expert_rows, w_up, preferred_element_type=jnp.float32)
    gate_sum, up_sum = (
        lax.psum_scatter(gate_part, "tensor", scatter_dimension=1, tiled=True),
        lax.psum_scatter(up_part, "tensor", scatter_dimension=1, tiled=True),
    )
    hidden_share = (jax.nn.silu(gate_sum) * up_sum).astype(jnp.bfloat16)
    hidden = lax.all_gather(hidden_share, "tensor", axis=1, tiled=True)
    partial_value = jnp.einsum("lrf,lfd->lrd", hidden, w_down, preferred_element_type=jnp.float32)
    outputs = lax.psum_scatter(partial_value, "dp", scatter_dimension=1, tiled=True)
    backward = outputs.reshape(local_experts, cap_share, expert_count, feature_cols)
    returned = lax.all_to_all(backward, "expert", split_axis=2, concat_axis=2, tiled=True)
    table_cols = local_experts * cap_share * expert_count
    returned = returned.reshape(table_cols, feature_cols)
    block_index = lax.axis_index("dp")
    is_mine = (slot_rank // cap_share == block_index).astype(jnp.float32)
    position = (within * cap_share + slot_rank % cap_share) * expert_count + owner_device
    scaled = gate_weights.reshape(-1) * is_mine
    combine_table = jnp.where(
        position[:, None] == lax.iota(jnp.int32, table_cols)[None, :], scaled[:, None], 0.0
    )
    combine_table = jnp.sum(combine_table.reshape(tok_rows, TOP, table_cols), axis=1)
    partial_mix = jnp.dot(
        combine_table, returned, precision=lax.Precision.HIGHEST, preferred_element_type=jnp.float32
    )
    mixed = lax.psum(partial_mix, "dp")
    return mixed.astype(jnp.bfloat16)


def solution(mesh):
    in_specs = (
        P("expert", "tensor"),
        P("expert", None),
        P("expert", None),
        P("expert", "tensor", "dp"),
        P("expert", "tensor", "dp"),
        P("expert", "dp", "tensor"),
    )
    out_specs = P("expert", "tensor")
    return jax.shard_map(
        per_device, mesh=mesh, in_specs=in_specs, out_specs=out_specs, check_vma=False
    )
```

profile of v0, /device:TPU:0, one launch (start us, length us, event | category | flops | bytes accessed | tf_op | source)
XLA Modules:
  0.0 219.1 jit_solution(13099469717093298027)
XLA Ops:
  6.5 0.0 copy-start
  6.5 0.0 reduce-scatter.4.cloned.1.call-start
  6.5 0.8 copy.43
  7.3 0.1 eq.66
  7.5 0.6 reduce-window.6
  8.1 0.2 slice_reduce_fusion
  8.3 0.1 bitcast_bitcast_fusion
  8.4 0.1 reduce_sum.30
  8.6 0.1 convert_reduce_fusion
  8.7 0.0 copy-done
  8.7 1.9 convolution_convert_fusion
  10.6 3.1 %reshape.151 = bf16[16,4,4,3584]{3,2,1,0:T(4,128)(2,1)S(1)} reshape(bf16[256,3584]{1,0:T(8,128)(2,1)} %convolution_convert_fusion) | data formatting | bytes 3670016 | tf_op jit(solution)/shard_map/reshape | solution.py:35
  13.8 0.7 copy.51
  14.5 48.7 %all_to_all.10 = bf16[16,4,4,3584]{3,1,0,2:T(4,128)(2,1)S(1)} all-to-all(bf16[16,4,4,3584]{3,1,0,2:T(4,128)(2,1)S(1)} %copy.51), channel_id=1, replica_groups=mesh['dp'=4,'expert'=4,'tensor'=2] {'expert'}, dimensions={2} | all-to-all | bytes 3670016 | tf_op jit(solution)/shard_map/all_to_all | solution.py:36
  63.2 2.7 %copy.52 = bf16[16,4,4,3584]{3,2,1,0:T(4,128)(2,1)} copy(bf16[16,4,4,3584]{3,1,0,2:T(4,128)(2,1)S(1)} %all_to_all.10) | data formatting | bytes 3670016 | tf_op jit(solution)/shard_map/all_to_all | solution.py:36
  65.9 2.9 %reshape.152 = bf16[16,16,3584]{2,1,0:T(8,128)(2,1)S(1)} reshape(bf16[16,4,4,3584]{3,2,1,0:T(4,128)(2,1)} %copy.52) | data formatting | bytes 3670016 | tf_op jit(solution)/shard_map/reshape | solution.py:37
  68.8 12.1 %fusion.7 = f32[16,16,256]{2,1,0:T(8,128)} fusion(bf16[16,16,3584]{2,1,0:T(8,128)(2,1)S(1)} %reshape.152, bf16[16,3584,256]{2,1,0:T(8,128)(2,1)} %param.9), kind=kOutput, calls=%fused_computation.29 | convolution fusion | flops 469762048 | bytes 31457280 | tf_op jit(solution)/shard_map/lrd,ldf->lrf/dot_general | solution.py:38
  80.9 0.0 reduce-scatter.4.cloned.1.call-update
  80.9 0.0 reduce-scatter.6.cloned.1.call-start
  81.0 12.2 %fusion.8 = f32[16,16,256]{2,1,0:T(8,128)} fusion(bf16[16,16,3584]{2,1,0:T(8,128)(2,1)S(1)} %reshape.152, bf16[16,3584,256]{2,1,0:T(8,128)(2,1)} %param.10), kind=kOutput, calls=%fused_computation.30 | convolution fusion | flops 469762048 | bytes 31457280 | tf_op jit(solution)/shard_map/lrd,ldf->lrf/dot_general | solution.py:39
  93.1 0.0 reduce-scatter.6.cloned.1.call-update
  93.2 0.0 reduce-scatter.8.cloned.1.call-start
  93.2 0.0 reduce-scatter.4.cloned.1.call-done
  93.2 12.8 %reduce-scatter.6.cloned.1.call-done = f32[16,8,256]{2,1,0:T(8,128)} async-done(((f32[16,16,256]{2,1,0:T(8,128)}), f32[16,8,256]{2,1,0:T(8,128)}) %reduce-scatter.6.cloned.1.call-update) | async-done | bytes 131088 | tf_op jit(solution)/shard_map/reduce_scatter | solution.py:42
  106.0 1.0 multiply_convert_fusion
  107.0 5.1 %all_gather.3 = bf16[16,16,256]{2,1,0:T(8,128)(2,1)S(1)} all-gather(bf16[16,8,256]{2,1,0:T(8,128)(2,1)S(1)} %multiply_convert_fusion), channel_id=1, replica_groups=mesh['dp'=4,'expert'=4,'tensor'=2] {'tensor'}, dimensions={1}, use_global_device_ids=true | all-gather | bytes 196608 | tf_op jit(solution)/shard_map/all_gather | solution.py:45
  112.2 11.4 %fusion.9 = f32[16,16,3584]{2,1,0:T(8,128)S(1)} fusion(bf16[16,16,256]{2,1,0:T(8,128)(2,1)S(1)} %all_gather.3, bf16[16,256,3584]{2,1,0:T(8,128)(2,1)} %param.11), kind=kOutput, calls=%fused_computation.31 | convolution fusion | flops 469762048 | bytes 33161216 | tf_op jit(solution)/shard_map/lrf,lfd->lrd/dot_general | solution.py:46
  123.5 3.9 %copy.53 = f32[16,16,3584]{2,0,1:T(8,128)} copy(f32[16,16,3584]{2,1,0:T(8,128)S(1)} %fusion.9) | data formatting | bytes 7340032 | tf_op jit(solution)/shard_map/lrf,lfd->lrd/dot_general | solution.py:46
  127.5 0.0 copy-start.2
  127.5 0.0 reduce-scatter.8.cloned.1.call-update
  127.5 41.4 %reduce-scatter.8.cloned.1.call-done = f32[16,4,3584]{2,0,1:T(8,128)} async-done(((f32[16,16,3584]{2,0,1:T(8,128)}), f32[16,4,3584]{2,0,1:T(8,128)}) %reduce-scatter.8.cloned.1.call-update) | async-done | bytes 917520 | tf_op jit(solution)/shard_map/reduce_scatter | solution.py:47
  168.9 0.0 copy-start.1
  168.9 4.7 %all-to-all-start.1 = ((f32[16,1,4,3584]{3,0,1,2:T(8,128)}), f32[16,1,4,3584]{3,0,1,2:T(8,128)S(1)}, u32[]{:S(2)}, u32[]{:S(2)}) async-start(f32[16,1,4,3584]{3,0,1,2:T(8,128)} %bitcast.27), calls=%async_computation.4 | async-start | bytes 1835008 | tf_op jit(solution)/shard_map/all_to_all | solution.py:49
  173.6 0.0 copy-done.2
  173.6 0.1 copy.50
  173.7 0.1 select_reduce_fusion
  173.9 22.5 %all-to-all-done.1 = f32[16,1,4,3584]{3,0,1,2:T(8,128)S(1)} async-done(((f32[16,1,4,3584]{3,0,1,2:T(8,128)}), f32[16,1,4,3584]{3,0,1,2:T(8,128)S(1)}, u32[]{:S(2)}, u32[]{:S(2)}) %all-to-all-start.1) | async-done | bytes 917536 | tf_op jit(solution)/shard_map/all_to_all | solution.py:49
  196.4 0.6 copy.55
  197.0 0.3 reshape.154
  197.3 0.6 fusion.10
  197.9 14.7 %all-reduce.2 = bf16[24,3584]{1,0:T(8,128)(2,1)} all-reduce(f32[24,3584]{1,0:T(8,128)S(1)} %fusion.10), channel_id=1, replica_groups=mesh['dp'=4,'expert'=4,'tensor'=2] {'dp'}, use_global_device_ids=true, to_apply=%region_8.9 | all-reduce | flops 86016 | bytes 516096 | tf_op jit(solution)/shard_map/psum | solution.py:63
  212.6 0.0 copy-done.1
  (7 shorter events, 0.1 us)
Async XLA Ops:
  6.5 2.2 copy-start
  6.5 86.7 %reduce-scatter.4.cloned.1.call-start = ((), (), s32[]{:S(2)}) async-start(), calls=%async_computation.5 | async-start | bytes 393216 | tf_op jit(solution)/shard_map/reduce_scatter | solution.py:41
  80.9 25.1 %reduce-scatter.6.cloned.1.call-start = ((), (), s32[]{:S(2)}) async-start(), calls=%async_computation.6 | async-start | bytes 393216 | tf_op jit(solution)/shard_map/reduce_scatter | solution.py:42
  93.2 75.8 %reduce-scatter.8.cloned.1.call-start = ((), (), s32[]{:S(2)}) async-start(), calls=%async_computation.7 | async-start | bytes 4587520 | tf_op jit(solution)/shard_map/reduce_scatter | solution.py:47
  127.5 46.2 %copy-start.2 = (f32[24,8]{0,1:T(8,128)S(1)}, f32[24,8]{0,1:T(8,128)}, u32[]{:S(2)}) copy-start(f32[24,8]{0,1:T(8,128)} %param.8) | copy-start | bytes 2308
  168.9 43.7 %copy-start.1 = (bf16[24,3584]{1,0:T(8,128)(2,1)S(1)}, bf16[24,3584]{1,0:T(8,128)(2,1)}, u32[]{:S(2)}) copy-start(bf16[24,3584]{1,0:T(8,128)(2,1)} %param.6) | copy-start | bytes 516100
  168.9 27.5 %all-to-all-start.1 = ((f32[16,1,4,3584]{3,0,1,2:T(8,128)}), f32[16,1,4,3584]{3,0,1,2:T(8,128)S(1)}, u32[]{:S(2)}, u32[]{:S(2)}) async-start(f32[16,1,4,3584]{3,0,1,2:T(8,128)} %bitcast.27), calls=%async_computation.4 | async-start | bytes 1835008 | tf_op jit(solution)/shard_map/all_to_all | solution.py:49
Sparse Core Ops, SparseCore 0:
  81.0 10.9 reduce-scatter.3
  94.2 11.7 reduce-scatter.5
  127.6 41.2 reduce-scatter.7
where the time goes:
time: 220 us; the launch traced here: 219 us
  waiting for transfers between devices  76.8 us (35%)
  blocking collectives  68.6 us (31%)
  matrix products  38.1 us (17%)
  local copies, waits for them, and re-layouts  15.5 us (7%)
  between operations  13.2 us (6%)
  starting transfers between devices  4.8 us (2%)
    all_to_all x1, blocking collectives, per_device(): lax.all_to_all(outbound, 'expert', split_axis=2, concat_axis=2, tiled=True)  48.7 us
    reduce_scatter x1, waiting for transfers between devices, per_device(): lax.psum_scatter(partial_value, 'dp', scatter_dimension=1, tiled=True)  41.4 us
    all_to_all x1, waiting for transfers between devices, per_device(): lax.all_to_all(backward, 'expert', split_axis=2, concat_axis=2, tiled=True)  22.5 us
    psum x1, blocking collectives, per_device(): mixed = lax.psum(partial_mix, 'dp')  14.7 us
    reduce_scatter x1, waiting for transfers between devices, per_device(): lax.psum_scatter(up_part, 'tensor', scatter_dimension=1, tiled=True)  12.8 us
    dot_general x1, matrix products, per_device(): jnp.einsum('lrd,ldf->lrf', expert_rows, w_up, preferred_element_type=jnp....  12.2 us
    dot_general x1, matrix products, per_device(): jnp.einsum('lrd,ldf->lrf', expert_rows, w_gate, preferred_element_type=jn...  12.1 us
    dot_general x1, matrix products, per_device(): jnp.einsum('lrf,lfd->lrd', hidden, w_down, preferred_element_type=jnp.flo...  11.4 us
  transfers between devices with their start and end apart: 4, of which 3 were waited for; matrix products, arithmetic and copies ran while one was open for 6% of the time, Pallas kernels for 0%

commit v1 on v0

v1 whole, which is shorter than its diff:
```python
import functools

import jax
import jax.numpy as jnp
from jax import lax
from jax.experimental import pallas as pl
from jax.experimental.pallas import tpu as pltpu
from jax.sharding import PartitionSpec as P

CAP = 4
LANES = 128
WEIGHT_VMEM = 57_500_000
VMEM_LIMIT = 67_043_328
DOWN_SLOTS = 8
HIDDEN_LAG = 4
MESH = pl.DeviceIdType.MESH
BF16, F32, I32 = jnp.bfloat16, jnp.float32, jnp.int32


def layer_kernel(
    cfg, tok_hbm, ids_hbm, gw_hbm, wg_hbm, wu_hbm, wd_hbm, out_ref,
    wg, wu, wd, tok, ids, gw, table, scale, rows_x, snd, rcv, dense,
    rs_buf, rs_recv, ex_send, ex_recv, ag,
    gu_sem, wd_sem, loc_sem, tok_send, tok_recv, rel_send, rel_recv, ids_send, ids_recv, gw_send, gw_recv,
    gu_send, gu_recv, rs_ssem, rs_rsem, ex_ssem, ex_rsem, ag_ssem, ag_rsem,
):
    n_e, n_d, n_t = cfg["n_e"], cfg["n_d"], cfg["n_t"]
    experts, width, hid = cfg["experts"], cfg["width"], cfg["hid"]
    t_dev, t_pad, top = cfg["t_dev"], cfg["t_pad"], cfg["top"]
    ng, nd, chunk, chunks = cfg["ng"], cfg["nd"], cfg["chunk"], cfg["chunks"]
    part = chunk // n_d
    slots = n_e * CAP
    all_slots = experts * slots
    me_e, me_d, me_t = lax.axis_index("expert"), lax.axis_index("dp"), lax.axis_index("tensor")

    next_e, next_d = lax.rem(me_e + 1, n_e), lax.rem(me_d + 1, n_d)

    def gate_copy(e, slot):
        return pltpu.make_async_copy(wg_hbm.at[e], wg.at[slot], gu_sem.at[0, slot])

    def up_copy(e, slot):
        return pltpu.make_async_copy(wu_hbm.at[e], wu.at[slot], gu_sem.at[1, slot])

    def down_copy(c, slot):
        cols = pl.ds(c * chunk if isinstance(c, int) else pl.multiple_of(c * chunk, LANES), chunk)
        return pltpu.make_async_copy(wd_hbm.at[:, :, cols], wd.at[slot], wd_sem.at[slot])

    def remote(src, dst, ssem, rsem, **where):
        return pltpu.make_async_remote_copy(
            src_ref=src, dst_ref=dst, send_sem=ssem, recv_sem=rsem, device_id=where, device_id_type=MESH
        )

    own_rows = pl.ds(0, t_dev)
    local = (
        pltpu.make_async_copy(ids_hbm, ids.at[0], loc_sem.at[0]),
        pltpu.make_async_copy(gw_hbm, gw.at[0], loc_sem.at[1]),
        pltpu.make_async_copy(tok_hbm, tok.at[0, own_rows], loc_sem.at[2]),
    )
    for copy in local:
        copy.start()
    for e in range(ng):
        gate_copy(e, e).start(priority=1)
        up_copy(e, e).start(priority=1)
    for k in range(nd):
        down_copy(k, k).start(priority=1)

    barrier = pltpu.get_barrier_semaphore()
    for axis, me, n in (("expert", me_e, n_e), ("dp", me_d, n_d), ("tensor", me_t, n_t)):
        for o in range(1, n):
            pl.semaphore_signal(barrier, inc=1, device_id={axis: lax.rem(me + o, n)}, device_id_type=MESH)
    pl.semaphore_wait(barrier, n_e + n_d + n_t - 3)

    half = width // 2
    mine = pl.ds(pl.multiple_of(lax.rem(me_d, 2) * half, LANES), half)
    theirs = pl.ds(pl.multiple_of((1 - lax.rem(me_d, 2)) * half, LANES), half)
    partner = me_d + 1 - 2 * lax.rem(me_d, 2)
    for copy in local:
        copy.wait()
    ids_out, gw_out, tok_out, rel_out = [], [], [], []
    for o in range(1, n_e):
        to = lax.rem(me_e + o, n_e)
        ids_out.append(remote(ids.at[0], ids.at[o], ids_send.at[o - 1], ids_recv.at[o - 1], expert=to))
        gw_out.append(remote(gw.at[0], gw.at[o], gw_send.at[o - 1], gw_recv.at[o - 1], expert=to))
        tok_out.append(
            remote(
                tok.at[0, own_rows, mine], tok.at[o, own_rows, mine], tok_send.at[o - 1], tok_recv.at[o - 1], expert=to
            )
        )
        rel_out.append(
            remote(
                tok.at[o, own_rows, mine], tok.at[o, own_rows, mine], rel_send.at[o - 1], rel_recv.at[o - 1], dp=partner
            )
        )
    for copy in ids_out + gw_out + tok_out:
        copy.start()

    if t_pad > t_dev:
        for p in range(n_e):
            tok[p, t_dev:t_pad, :] = jnp.zeros((t_pad - t_dev, width), BF16)
    lane = lax.broadcasted_iota(I32, (t_dev, all_slots), 1)
    lane_expert = lane // slots + me_e * experts
    lane_slot = lane % slots
    earlier = (
        lax.broadcasted_iota(I32, (t_dev, t_dev), 1) < lax.broadcasted_iota(I32, (t_dev, t_dev), 0)
    ).astype(F32).astype(BF16)
    picks, weights = [], []
    for p in range(n_e):
        if p > 0:
            ids_out[p - 1].wait_recv()
            gw_out[p - 1].wait_recv()
        named = jnp.zeros((t_dev, all_slots), F32)
        weight = jnp.zeros((t_dev, all_slots), F32)
        ids_p, gw_p = ids[p], gw[p]
        for k in range(top):
            hit = ids_p[:, k : k + 1] == lane_expert
            named = jnp.where(hit, 1.0, named)
            weight = jnp.where(hit, gw_p[:, k : k + 1], weight)
        rank = jnp.dot(earlier, named.astype(BF16), preferred_element_type=F32)
        at = (rank + p * CAP).astype(I32)
        pick = jnp.where(at == lane_slot, named, 0.0)
        rest = jnp.zeros((t_pad - t_dev, all_slots), F32)
        picks += [pick, rest]
        weights += [pick * weight, rest]
    table[...] = jnp.concatenate(picks, axis=0).T.astype(BF16)
    slot_weight = jnp.sum(jnp.concatenate(weights, axis=0).T, axis=1, keepdims=True)
    scale[...] = jnp.broadcast_to(slot_weight, (all_slots, hid))

    for o in range(1, n_e):
        tok_out[o - 1].wait_recv()
        rel_out[o - 1].start()
    for o in range(1, n_e):
        remote(
            tok.at[o, own_rows, theirs], tok.at[o, own_rows, theirs], rel_send.at[o - 1], rel_recv.at[o - 1], dp=partner
        ).wait_recv()

    @pl.loop(0, chunks)
    def _(c):
        cols = pl.ds(pl.multiple_of(c * chunk, LANES), chunk)
        feed = tok[:, :, cols].reshape(n_e * t_pad, chunk)
        rows_x[:, cols] = jnp.dot(table[...], feed, preferred_element_type=F32).astype(BF16)

    def partial_copy(e, o):
        return remote(
            snd.at[e], rcv.at[o - 1, e], gu_send.at[o - 1, e], gu_recv.at[o - 1, e], tensor=lax.rem(me_t + o, n_t)
        )

    def finish_hidden(e):
        total = snd[e]
        for o in range(1, n_t):
            partial_copy(e, o).wait_recv()
            total = total + rcv[o - 1, e]
        gate, up = total[:, :hid], total[:, hid:]
        rows = pl.ds(pl.multiple_of(e * slots, slots), slots)
        hidden = (gate / (1.0 + jnp.exp(-gate)) * up * scale[rows, :]).astype(BF16)
        spread = lax.dot_general(
            table[rows, :], hidden, (((0,), (0,)), ((), ())), preferred_element_type=F32
        )
        if t_pad > t_dev:
            spread = spread.reshape(n_e, t_pad, hid)[:, :t_dev, :].reshape(n_e * t_dev, hid)
        dense[:, pl.ds(pl.multiple_of(e * hid, hid), hid)] = spread.astype(BF16)

    @pl.loop(0, experts)
    def _(e):
        slot = lax.rem(e, ng)
        rows = pl.ds(pl.multiple_of(e * slots, slots), slots)
        x = rows_x[rows, :]
        gate_copy(e, slot).wait()
        gate = jnp.dot(x, wg[slot], preferred_element_type=F32)
        up_copy(e, slot).wait()
        up = jnp.dot(x, wu[slot], preferred_element_type=F32)
        snd[e, :, :hid] = gate
        snd[e, :, hid:] = up

        @pl.when(e + ng < experts)
        def _():
            gate_copy(e + ng, slot).start(priority=1)
            up_copy(e + ng, slot).start(priority=1)

        for o in range(1, n_t):
            partial_copy(e, o).start()

        @pl.when(e >= HIDDEN_LAG)
        def _():
            finish_hidden(e - HIDDEN_LAG)

    @pl.loop(max(experts - HIDDEN_LAG, 0), experts)
    def _(e):
        finish_hidden(e)

    def send_dp(c):
        for o in range(1, n_d):
            d = lax.rem(me_d + o, n_d)
            remote(rs_buf.at[c, d], rs_recv.at[c, o - 1], rs_ssem.at[c], rs_rsem.at[c], dp=d).start()

    def whole_dp(c):
        return remote(rs_buf.at[c, pl.ds(0, n_d - 1)], rs_recv.at[c], rs_ssem.at[c], rs_rsem.at[c], dp=next_d)

    def whole_ex(c):
        return remote(ex_send.at[c, pl.ds(1, n_e - 1)], ex_recv.at[c], ex_ssem.at[c], ex_rsem.at[c], expert=next_e)

    def whole_ag(c):
        span = ag.at[c, pl.ds(0, n_d - 1)]
        return remote(span, span, ag_ssem.at[c], ag_rsem.at[c], dp=next_d)

    def reduce_dp(c):
        whole_dp(c).wait_recv()
        total = rs_buf[c, me_d].astype(F32)
        for o in range(1, n_d):
            total = total + rs_recv[c, o - 1].astype(F32)
        for p in range(n_e):
            ex_send[c, p] = total[p * t_dev : (p + 1) * t_dev, :].astype(BF16)
        for p in range(1, n_e):
            to = lax.rem(me_e + n_e - p, n_e)
            remote(ex_send.at[c, p], ex_recv.at[c, p - 1], ex_ssem.at[c], ex_rsem.at[c], expert=to).start()

    def reduce_ex(c):
        whole_ex(c).wait_recv()
        total = ex_send[c, 0].astype(F32)
        for p in range(1, n_e):
            total = total + ex_recv[c, p - 1].astype(F32)
        ag[c, me_d] = total.astype(BF16)
        for o in range(1, n_d):
            d = lax.rem(me_d + o, n_d)
            remote(ag.at[c, me_d], ag.at[c, me_d], ag_ssem.at[c], ag_rsem.at[c], dp=d).start()

    def finish(c):
        whole_ag(c).wait_recv()
        for q in range(n_d):
            first = c * chunk + q * part
            out_ref[:, first : first + part] = ag[c, q]

    for c in range(chunks):
        slot = c % nd
        down_copy(c, slot).wait()
        acc = jnp.dot(
            dense[...], wd[slot].reshape(experts * hid, chunk), preferred_element_type=F32
        )
        for q in range(n_d):
            rs_buf[c, q] = acc[:, q * part : (q + 1) * part].astype(BF16)
        if c + nd < chunks:
            down_copy(c + nd, slot).start(priority=1)
        send_dp(c)
        if c >= 2:
            reduce_dp(c - 2)
        if c >= 5:
            reduce_ex(c - 5)
    for c in range(max(chunks - 2, 0), chunks):
        reduce_dp(c)
    for c in range(max(chunks - 5, 0), chunks):
        reduce_ex(c)
    for c in range(chunks):
        finish(c)

    for copy in ids_out + gw_out + tok_out + rel_out:
        copy.wait_send()

    @pl.loop(0, experts)
    def _(e):
        for o in range(1, n_t):
            partial_copy(e, o).wait_send()

    for c in range(chunks):
        whole_dp(c).wait_send()
        whole_ex(c).wait_send()
        whole_ag(c).wait_send()


def per_device(cfg, tokens, expert_ids, gate_weights, w_gate, w_up, w_down):
    n_e, n_d, n_t = cfg["n_e"], cfg["n_d"], cfg["n_t"]
    t_dev, width = tokens.shape
    top = expert_ids.shape[1]
    experts, _, hid = w_gate.shape
    t_pad = -(-t_dev // 16) * 16
    chunk = n_d * LANES
    while width % chunk:
        chunk -= LANES
    chunks = width // chunk
    nd = min(DOWN_SLOTS, chunks)
    room = WEIGHT_VMEM - nd * experts * hid * chunk * 2
    ng = max(1, min(experts, room // (width * hid * 4)))
    part = chunk // n_d
    slots = n_e * CAP
    cfg = dict(
        cfg, experts=experts, width=width, hid=hid, t_dev=t_dev, t_pad=t_pad, top=top,
        ng=ng, nd=nd, chunk=chunk, chunks=chunks,
    )
    dma, vmem = pltpu.SemaphoreType.DMA, pltpu.VMEM
    scratch = [
        vmem((ng, width, hid), BF16),
        vmem((ng, width, hid), BF16),
        vmem((nd, experts, hid, chunk), BF16),
        vmem((n_e, t_pad, width), BF16),
        vmem((n_e, t_dev, top), I32),
        vmem((n_e, t_dev, top), F32),
        vmem((experts * slots, n_e * t_pad), BF16),
        vmem((experts * slots, hid), F32),
        vmem((experts * slots, width), BF16),
        vmem((experts, slots, 2 * hid), F32),
        vmem((n_t - 1, experts, slots, 2 * hid), F32),
        vmem((n_e * t_dev, experts * hid), BF16),
        vmem((chunks, n_d, n_e * t_dev, part), BF16),
        vmem((chunks, n_d - 1, n_e * t_dev, part), BF16),
        vmem((chunks, n_e, t_dev, part), BF16),
        vmem((chunks, n_e - 1, t_dev, part), BF16),
        vmem((chunks, n_d, t_dev, part), BF16),
        dma((2, ng)), dma((nd,)), dma((3,)),
        dma((n_e - 1,)), dma((n_e - 1,)), dma((n_e - 1,)), dma((n_e - 1,)),
        dma((n_e - 1,)), dma((n_e - 1,)), dma((n_e - 1,)), dma((n_e - 1,)),
        dma((n_t - 1, experts)), dma((n_t - 1, experts)),
        dma((chunks,)), dma((chunks,)), dma((chunks,)), dma((chunks,)), dma((chunks,)), dma((chunks,)),
    ]
    anywhere = pl.BlockSpec(memory_space=pl.ANY)
    return pl.pallas_call(
        functools.partial(layer_kernel, cfg),
        out_shape=jax.ShapeDtypeStruct((t_dev, width), BF16),
        in_specs=[anywhere] * 6,
        out_specs=pl.BlockSpec(memory_space=vmem),
        scratch_shapes=scratch,
        compiler_params=pltpu.CompilerParams(
            collective_id=0, has_side_effects=True, vmem_limit_bytes=VMEM_LIMIT
        ),
    )(tokens, expert_ids, gate_weights, w_gate, w_up, w_down)


def solution(mesh):
    cfg = {"n_e": mesh.shape["expert"], "n_d": mesh.shape["dp"], "n_t": mesh.shape["tensor"]}
    in_specs = (
        P("expert", "tensor"),
        P("expert", None),
        P("expert", None),
        P("expert", "tensor", "dp"),
        P("expert", "tensor", "dp"),
        P("expert", "dp", "tensor"),
    )
    return jax.shard_map(
        functools.partial(per_device, cfg), mesh=mesh, in_specs=in_specs,
        out_specs=P("expert", "tensor"), check_vma=False,
    )
```

time: 220 us -> 66.8 us (0.30)
  waiting for transfers between devices: 76.8 us -> 0 us
  blocking collectives: 68.6 us -> 0 us
  Pallas kernels: 0 us -> 62.3 us
  matrix products: 38.1 us -> 0 us
  between operations: 13.2 us -> 0.01 us
  local copies, waits for them, and re-layouts: 15.5 us -> 4.31 us
  starting transfers between devices: 4.8 us -> 0 us
    pallas_call x0 -> x1, Pallas kernels: none -> 62.3 us  [per_device(): pl.pallas_call(functools.partial(layer_kernel, cfg), out_shape=jax.ShapeD...]
    reduce_scatter x3 -> x0, waiting for transfers between devices: 54.2 us -> none  [the longest x1 41.4 us: per_device(): lax.psum_scatter(partial_value, 'dp', scatter_dimension=1, tiled=True)]
    all_to_all x1 -> x0, blocking collectives: 48.7 us -> none  [per_device(): lax.all_to_all(outbound, 'expert', split_axis=2, concat_axis=2, tiled=True)]
    dot_general x5 -> x0, matrix products: 38.1 us -> none  [the longest x1 12.2 us: per_device(): jnp.einsum('lrd,ldf->lrf', expert_rows, w_up, preferred_element_type=jnp....]
    all_to_all x1 -> x0, waiting for transfers between devices: 22.5 us -> none  [per_device(): lax.all_to_all(backward, 'expert', split_axis=2, concat_axis=2, tiled=True)]
    psum x1 -> x0, blocking collectives: 14.7 us -> none  [per_device(): mixed = lax.psum(partial_mix, 'dp')]
    reshape x4 -> x0, local copies, waits for them, and re-layouts: 7.08 us -> none  [the longest x2 3.83 us: per_device(): outbound = outbound.reshape(local_experts, CAP, expert_count, feature_cols)]
    all_gather x1 -> x0, blocking collectives: 5.11 us -> none  [per_device(): hidden = lax.all_gather(hidden_share, 'tensor', axis=1, tiled=True)]
  transfers between devices with their start and end apart: 4 -> 0, of which waited for: 3 -> 0; matrix products, arithmetic and copies ran while one was open for 6% -> 0% of each run, Pallas kernels for 0% -> 0%
where the time goes in v1:
time: 66.8 us; the launch traced here: 66.6 us
  Pallas kernels  62.3 us (93%)
  local copies, waits for them, and re-layouts  4.31 us (6%)
    pallas_call x1, Pallas kernels, per_device(): pl.pallas_call(functools.partial(layer_kernel, cfg), out_shape=jax.ShapeD...  62.3 us
    unnamed x3, local copies, waits for them, and re-layouts  4.31 us

profile of v1, /device:TPU:0, one launch (start us, length us, event | category | flops | bytes accessed | tf_op | source)
XLA Modules:
  0.0 66.6 jit_solution(13169822984851820195)
XLA Ops:
  0.0 1.4 %copy.7.ids_hbm = s32[24,8]{1,0:T(8,128)} copy(s32[24,8]{0,1:T(8,128)} %param.7) | data formatting | bytes 1536 | tf_op args[1]
  1.4 1.4 %copy.8.gw_hbm = f32[24,8]{1,0:T(8,128)} copy(f32[24,8]{0,1:T(8,128)} %param.8) | data formatting | bytes 1536 | tf_op args[2]
  2.7 62.3 %shard_map.64 = bf16[24,3584]{1,0:T(8,128)(2,1)} custom-call(bf16[24,3584]{1,0:T(8,128)(2,1)} %tok_hbm.1, s32[24,8]{1,0:T(8,128)} %copy.7.ids_hbm, f32[24,8]{1,0:T(8,128)} %copy.8.gw_hbm, bf16[16,3584,256]{2,1,0:T(8,128)(2,1)} %wg_hbm.1, bf16[16,3584,256]{2,1,0:T(8,128)(2,1)} %wu_hbm.1, bf16[16,256,3584]{2,1,0:T(8,128)(2,1)} %wd_hbm.1), custom_call_target="tpu_custom_call" | custom-call | tf_op jit(solution)/shard_map/pallas_call | solution.py:313
  65.0 1.6 %copy.10 = bf16[24,3584]{1,0:T(8,128)(2,1)} copy(bf16[24,3584]{1,0:T(8,128)(2,1)} %shard_map.64) | data formatting | bytes 344064
